TPU v7x, 32 devices: a whole 2x2x4 slice. The times are simulated.
32 devices in a mesh: dp: 4 (over y, x), tensor: 8 (over z, core).
Axes of the slice: x: 2, y: 2, z: 4, core: 2. Of those that a mesh axis runs over, the one named last changes fastest.
Arguments:
- saved_input: bfloat16 [512, 8192], P(('dp', 'tensor')), may hold values from -8 to 8
- keep_bits: int32 [512, 448], P(('dp', 'tensor')), may hold values from -2147483648 to 2147483646, as said below
- norm_gain: bfloat16 [8192], P('dp'), may hold values from 0.099609375 to 1.8984375
- gate_weight: bfloat16 [8192, 14336], P('dp', 'tensor'), may hold values from -0.0625 to 0.0625
- up_weight: bfloat16 [8192, 14336], P('dp', 'tensor'), may hold values from -0.0625 to 0.0625
- down_weight: bfloat16 [14336, 8192], P('tensor', 'dp'), may hold values from -0.046875 to 0.046875
Outputs:
- layer_out: bfloat16 [512, 8192], P('tensor', 'dp')
- row_check: float32 [512], P('tensor')
Inputs may be any that keep to these rules, and one draw needn't show every extreme that they name: `keep_bits`: bit k of word w of a token is the keep bit of hidden unit 32 w + k.
All inputs are finite; a program needn't handle non-finite values.
Results may differ from a plain program's by a relative error of at most 0.017.
Values may be sent and summed in bfloat16 or wider, within the bound.
A program may use at most 64 MiB of HBM per device.

v0:
```python
import jax
import jax.numpy as jnp
from jax import lax
from jax.experimental import pallas as pl
from jax.experimental.pallas import tpu as pltpu
from jax.sharding import PartitionSpec as P

D = 8192


def on_device(saved_input, keep_bits, norm_gain, gate_weight, up_weight, down_weight):
    tensor_width = lax.axis_size("tensor")
    dp_width = lax.axis_size("dp")
    unit_words = lax.all_to_all(keep_bits, "tensor", split_axis=1, concat_axis=0, tiled=True)
    shifts = jnp.arange(32, dtype=jnp.int32)
    keep_mask = jnp.bitwise_and(jnp.right_shift(unit_words[:, :, None], shifts[None, None, :]), 1)
    keep_mask = keep_mask.reshape(unit_words.shape[0], -1)
    keep_scale = 2.0 * keep_mask.astype(jnp.float32)
    width_units = gate_weight.shape[1]
    columns = lax.all_to_all(saved_input, "dp", split_axis=1, concat_axis=0, tiled=True)
    collected = lax.all_gather(columns, "tensor", axis=0, tiled=True)
    per_device = saved_input.shape[0]
    collected = collected.reshape(tensor_width, dp_width, per_device, collected.shape[1])
    collected = collected.transpose(1, 0, 2, 3).reshape(-1, collected.shape[3])
    widened = collected.astype(jnp.float32)
    squares = lax.psum(jnp.sum(widened * widened, axis=1), "dp")
    inv_rms = lax.rsqrt(squares / D + 1e-05)
    normed = (widened * inv_rms[:, None] * norm_gain.astype(jnp.float32)[None, :]).astype(
        jnp.bfloat16
    )
    gate_part = jnp.dot(normed, gate_weight, preferred_element_type=jnp.float32)
    up_part = jnp.dot(normed, up_weight, preferred_element_type=jnp.float32)
    projected = lax.psum_scatter(
        jnp.concatenate((gate_part, up_part), axis=1).astype(jnp.bfloat16),
        "dp",
        scatter_dimension=0,
        tiled=True,
    ).astype(jnp.float32)
    gate_sum = projected[:, :width_units]
    up_sum = projected[:, width_units:]
    hidden = (jax.nn.silu(gate_sum) * up_sum * keep_scale).astype(jnp.bfloat16)
    partial_value = jnp.dot(
        lax.all_gather(hidden, "dp", axis=0, tiled=True),
        down_weight,
        preferred_element_type=jnp.float32,
    )
    mlp_sum = lax.psum_scatter(
        partial_value.astype(jnp.bfloat16), "tensor", scatter_dimension=0, tiled=True
    ).astype(jnp.float32)
    out_rows = mlp_sum.shape[0]
    first_row = lax.axis_index("tensor") * out_rows
    residual = lax.dynamic_slice_in_dim(collected, first_row, out_rows, 0)
    layer_out = (residual.astype(jnp.float32) + mlp_sum).astype(jnp.bfloat16)
    widened_out = layer_out.astype(jnp.float32)
    row_check = lax.psum(jnp.sum(widened_out * widened_out, axis=1), "dp") / D
    return (layer_out, row_check)


MESH = pl.DeviceIdType.MESH
F32 = jnp.float32
BF16 = jnp.bfloat16
COL_PARTS = 4


def fused(
    x_ref, kb_ref, gain_ref, wg_hbm, wu_hbm, wd_hbm, out_ref, chk_ref,
    wg, wu, wd, xbuf, xn, kw, kall, iown, iall, keep,
    pd, py, px, pown, relay, from_x, from_y, hbuf, qf, qb, sib, ssend, acc, zr, zpass, cown, call,
    w_sem, rx, tx_dp, tx_z, tx_s, rk, tk, ri, ti, rp, tp, rh, th, rs, ts, rz, rpass, tz, rc, tc,
):
    m, R = xbuf.shape[1], xbuf.shape[2]
    width = xbuf.shape[3]
    TB = m * R
    U = wg.shape[1]
    half_rows = out_ref.shape[0]
    words = kb_ref.shape[1] // m
    tile = 256 if U % 256 == 0 and width % 256 == 0 else 128
    step_cols = -(-(U // tile) // COL_PARTS) * tile
    parts = tuple((lo, min(step_cols, U - lo)) for lo in range(0, U, step_cols))

    i, j = lax.axis_index("dp"), lax.axis_index("tensor")
    iy, ix = i // 2, i % 2
    z, c = j // 2, j % 2
    xnb = iy * 2 + (1 - ix)
    ynb = (1 - iy) * 2 + ix
    diag = (1 - iy) * 2 + (1 - ix)
    sibling = z * 2 + (1 - c)
    mate = z + 1 - 2 * (z % 2)
    far, far_end = 2 - z // 2, 3 * (1 - z // 2)
    inner = (z + 1) // 2 == 1
    sends, inner_sends = [], []

    def send(src, dst, ss, rsem, to):
        copy = pltpu.make_async_remote_copy(
            src_ref=src, dst_ref=dst, send_sem=ss, recv_sem=rsem, device_id=to, device_id_type=MESH
        )
        copy.start()
        sends.append(copy)

    def arrived(dst, rsem):
        pltpu.make_async_remote_copy(
            src_ref=dst, dst_ref=dst, send_sem=tc.at[0], recv_sem=rsem,
            device_id=(i, sibling), device_id_type=MESH,
        ).wait_recv()

    loads = [pltpu.make_async_copy(s, d, w_sem.at[k]) for k, (s, d) in enumerate(((wg_hbm, wg), (wu_hbm, wu), (wd_hbm, wd)))]
    for load in loads:
        load.start()

    barrier = pltpu.get_barrier_semaphore()
    for other in (xnb, ynb, diag):
        pl.semaphore_signal(barrier, inc=1, device_id=(other, j), device_id_type=MESH)
    for step in range(1, m):
        pl.semaphore_signal(barrier, inc=1, device_id=(i, (j + step) % m), device_id_type=MESH)
    xbuf[i, j] = x_ref[:, pl.ds(pl.multiple_of(i * width, width), width)]
    pl.semaphore_wait(barrier, 3 + m - 1)

    for k, other in enumerate((diag, ynb, xnb)):
        send(x_ref.at[:, pl.ds(pl.multiple_of(other * width, width), width)], xbuf.at[i, j], tx_dp.at[k], rx.at[i, j], (other, j))

    kw[...] = jnp.zeros_like(kw)
    for t in range(m):
        kw[t, :, 0:words] = kb_ref[:, t * words : (t + 1) * words]
    rows = x_ref[...].astype(F32)
    total = jnp.sum(rows * rows, axis=1, keepdims=True)
    iown[...] = jnp.broadcast_to(lax.rsqrt(total / (x_ref.shape[1]) + 1e-05), iown.shape)
    iall[j] = iown[...]
    kall[j] = kw[j]

    order = (diag, ynb, xnb, i)
    for k, b in enumerate(order):
        if k < 3:
            arrived(xbuf.at[b, j], rx.at[b, j])
        for q, to in enumerate((mate, far)):
            send(xbuf.at[b, j], xbuf.at[b, j], tx_z.at[k, q], rx.at[b, j], (i, to * 2 + c))
        send(xbuf.at[b, j], xbuf.at[b, j], tx_s.at[k, 0], rx.at[b, j], (i, sibling))

    gain = gain_ref[...].astype(F32).reshape(1, width)

    def forward(k):
        b = order[k]
        for q, chip in enumerate((mate, far, far_end)):
            slot = chip * 2 + c
            arrived(xbuf.at[b, slot], rx.at[b, slot])
            if q > 0:
                copy = pltpu.make_async_remote_copy(
                    src_ref=xbuf.at[b, slot], dst_ref=xbuf.at[b, slot], send_sem=tx_z.at[k, q + 1],
                    recv_sem=rx.at[b, slot], device_id=(i, mate * 2 + c), device_id_type=MESH,
                )
                pl.when(inner)(copy.start)
                inner_sends.append(copy)
            send(xbuf.at[b, slot], xbuf.at[b, slot], tx_s.at[k, q + 1], rx.at[b, slot], (i, sibling))

    def collect(k):
        b = order[k]
        for chip in (z, mate, far, far_end):
            slot = chip * 2 + (1 - c)
            arrived(xbuf.at[b, slot], rx.at[b, slot])

        def scale(t, carry):
            xn[k, pl.ds(pl.multiple_of(t * R, R), R), :] = (xbuf[b, t].astype(F32) * gain).astype(BF16)
            return carry

        lax.fori_loop(0, m, scale, 0)

    def project(k, w, dst, lo=0, hi=U, extra=None):
        def body(t, carry):
            cols = pl.ds(pl.multiple_of(t * tile, tile), tile)
            part = jnp.dot(xn[k], w[:, cols], preferred_element_type=F32)
            if extra is not None:
                part = part + extra[:, cols].astype(F32)
            dst[:, cols] = part.astype(dst.dtype)
            return carry

        lax.fori_loop(lo // tile, hi // tile, body, 0)

    def stage(k, w, dst, to, land, slot):
        for p, (lo, size) in enumerate(parts):
            cols = pl.ds(lo, size)
            project(k, w, dst, lo, lo + size)
            send(dst.at[:, cols], land.at[:, cols], tp.at[p, slot], rp.at[p, slot], (to, j))

    forward(0)
    collect(0)
    loads[0].wait()
    loads[1].wait()
    for p, (lo, size) in enumerate(parts):
        cols = pl.ds(lo, size)
        project(0, wg, pd.at[0], lo, lo + size)
        send(pd.at[0, :, cols], relay.at[0, :, cols], tp.at[p, 0], rp.at[p, 0], (xnb, j))
        project(0, wu, pd.at[1], lo, lo + size)
        send(pd.at[1, :, cols], relay.at[1, :, cols], tp.at[p, 1], rp.at[p, 1], (ynb, j))
    forward(1)
    collect(1)
    stage(1, wu, py.at[1], ynb, from_y.at[1], 2)
    forward(2)
    collect(2)
    stage(2, wg, px.at[0], xnb, from_x.at[0], 3)
    forward(3)
    for p, (lo, size) in enumerate(parts):
        cols = pl.ds(lo, size)
        arrived(relay.at[0, :, cols], rp.at[p, 0])
        project(1, wg, py.at[0], lo, lo + size, relay.at[0])
        send(py.at[0, :, cols], from_y.at[0, :, cols], tp.at[p, 4], rp.at[p, 4], (ynb, j))
        arrived(relay.at[1, :, cols], rp.at[p, 1])
        project(2, wu, px.at[1], lo, lo + size, relay.at[1])
        send(px.at[1, :, cols], from_x.at[1, :, cols], tp.at[p, 5], rp.at[p, 5], (xnb, j))
    for step in range(1, m):
        to = (j + step) % m
        send(kw.at[to], kall.at[j], tk.at[step - 1], rk.at[j], (i, to))
        send(iown, iall.at[j], ti.at[step - 1], ri.at[j], (i, to))
    collect(3)
    project(3, wg, pown.at[0])
    project(3, wu, pown.at[1])

    for step in range(1, m):
        slot = (j + step) % m
        arrived(kall.at[slot], rk.at[slot])
        arrived(iall.at[slot], ri.at[slot])
    word = kall[...].reshape(TB, kall.shape[2])
    scale_rows = iall[...].reshape(TB, iall.shape[2])[:, 0:1]
    byte = [jnp.bitwise_and(jnp.right_shift(word, 8 * q), 255).astype(F32).astype(BF16) for q in range(4)]
    lanes = kall.shape[2]

    def expand(t, carry):
        unit = t * tile + lax.broadcasted_iota(jnp.int32, (lanes, tile), 1)
        where = lax.broadcasted_iota(jnp.int32, (lanes, tile), 0)
        spread = jnp.zeros((TB, tile), F32)
        for q in range(4):
            hit = (jnp.right_shift(unit, 3) == where * 4 + q)
            spread += jnp.dot(byte[q], jnp.where(hit, 1.0, 0.0).astype(BF16), preferred_element_type=F32)
        shift = jnp.bitwise_and(lax.broadcasted_iota(jnp.int32, (TB, tile), 1), 7)
        bit = jnp.bitwise_and(jnp.right_shift(spread.astype(jnp.int32), shift), 1)
        keep[:, pl.ds(pl.multiple_of(t * tile, tile), tile)] = (2 * bit).astype(F32)
        return carry

    lax.fori_loop(0, U // tile, expand, 0)

    for p, (lo, size) in enumerate(parts):
        cols = pl.ds(lo, size)
        arrived(from_y.at[1, :, cols], rp.at[p, 2])
        arrived(from_x.at[0, :, cols], rp.at[p, 3])
        arrived(from_y.at[0, :, cols], rp.at[p, 4])
        arrived(from_x.at[1, :, cols], rp.at[p, 5])

        def activate(t, carry):
            at = pl.ds(pl.multiple_of(t * tile, tile), tile)
            gate = (pown[0, :, at] + from_x[0, :, at].astype(F32) + from_y[0, :, at].astype(F32)) * scale_rows
            up = (pown[1, :, at] + from_x[1, :, at].astype(F32) + from_y[1, :, at].astype(F32)) * scale_rows
            hbuf[i, :, at] = (gate / (1.0 + jnp.exp(-gate)) * up * keep[:, at]).astype(BF16)
            return carry

        lax.fori_loop(lo // tile, (lo + size) // tile, activate, 0)
        send(hbuf.at[i, :, cols], hbuf.at[i, :, cols], th.at[p, 0], rh.at[i, p], (xnb, j))
        send(hbuf.at[i, :, cols], hbuf.at[i, :, cols], th.at[p, 1], rh.at[i, p], (ynb, j))

    loads[2].wait()
    blocks = (i, xnb, ynb, diag)

    span = width // 2
    halves = [pl.ds(h * span, span) for h in range(2)]

    def down(k, h):
        b = blocks[k]

        def body(t, carry):
            cols = pl.ds(pl.multiple_of(t * tile, tile), tile)
            part = jnp.dot(hbuf[b], wd[:, cols], preferred_element_type=F32)
            for r in range(2):
                piece = part[r * half_rows : (r + 1) * half_rows]
                qf[k, r, :, cols] = piece
                qb[k, r, :, cols] = piece.astype(BF16)
            return carry

        lax.fori_loop(h * span // tile, (h + 1) * span // tile, body, 0)
        at = halves[h]
        send(qb.at[k, 1 - c, :, at], sib.at[k, :, at], ts.at[k, h], rs.at[k, h], (i, sibling))

    away_sends = []

    def pair(k, h):
        b, at = blocks[k], halves[h]
        arrived(sib.at[k, :, at], rs.at[k, h])
        qf[k, c, :, at] = qf[k, c, :, at] + sib[k, :, at].astype(F32)
        here, near = b == z, b == mate
        away = b // 2 != z // 2
        outer = (z + 1) // 2 != 1

        def copy_to(dst, rsem, chip):
            return pltpu.make_async_remote_copy(
                src_ref=ssend.at[k, :, at], dst_ref=dst, send_sem=tz.at[k, h], recv_sem=rsem,
                device_id=(i, chip * 2 + c), device_id_type=MESH,
            )

        direct = copy_to(zr.at[0, :, at], rz.at[0, h], mate)
        passed = copy_to(zpass.at[b, :, at], rpass.at[b, h], mate)
        joined = copy_to(zr.at[1, :, at], rz.at[1, h], b)

        @pl.when(here)
        def _():
            acc[:, at] = qf[k, c, :, at]

        @pl.when(near)
        def _():
            ssend[k, :, at] = qf[k, c, :, at].astype(BF16)
            direct.start()

        @pl.when(jnp.logical_and(away, outer))
        def _():
            ssend[k, :, at] = qf[k, c, :, at].astype(BF16)
            passed.start()

        away_sends.append((here, away, direct, joined))

    def join(k, h):
        b, at = blocks[k], halves[h]
        _, away, _, joined = away_sends[2 * k + h]

        @pl.when(jnp.logical_and(away, inner))
        def _():
            arrived(zpass.at[b, :, at], rpass.at[b, h])
            ssend[k, :, at] = (qf[k, c, :, at] + zpass[b, :, at].astype(F32)).astype(BF16)
            joined.start()

    def hand_on(p):
        cols = pl.ds(parts[p][0], parts[p][1])
        src, to = ((xnb, ynb), (ynb, xnb))[p % 2]
        arrived(hbuf.at[src, :, cols], rh.at[src, p])
        send(hbuf.at[src, :, cols], hbuf.at[src, :, cols], th.at[p, 2], rh.at[src, p], (to, j))

    def rest(p, src):
        cols = pl.ds(parts[p][0], parts[p][1])
        arrived(hbuf.at[src, :, cols], rh.at[src, p])

    last = len(parts) - 1
    down(0, 0)
    hand_on(0)
    down(0, 1)
    pair(0, 0)
    for p in range(1, last):
        hand_on(p)
    pair(0, 1)
    hand_on(last)
    for p in range(1, last + 1, 2):
        rest(p, xnb)
    down(1, 0)
    down(1, 1)
    pair(1, 0)
    for p in range(0, last + 1, 2):
        rest(p, ynb)
    down(2, 0)
    pair(1, 1)
    join(0, 0)
    join(0, 1)
    down(2, 1)
    pair(2, 0)
    for p in range(last + 1):
        rest(p, diag)
    down(3, 0)
    pair(2, 1)
    down(3, 1)
    pair(3, 0)
    pair(3, 1)
    for k in range(1, 4):
        join(k, 0)
        join(k, 1)

    first = j * (half_rows // R)
    mine = xbuf.reshape(xbuf.shape[0] * m, R, width)
    value = acc[...]
    for slot in range(2):
        for h in range(2):
            arrived(zr.at[slot, :, halves[h]], rz.at[slot, h])
        value = value + zr[slot].astype(F32)
    acc[...] = value
    sums = []
    for q in range(half_rows // R):
        rows_q = pl.ds(q * R, R)
        result = (mine[first + q].astype(F32) + acc[rows_q, :]).astype(BF16)
        out_ref[rows_q, :] = result
        wide = result.astype(F32)
        cown[rows_q, :] = jnp.broadcast_to(jnp.sum(wide * wide, axis=1, keepdims=True), (R, cown.shape[1]))
    for k, other in enumerate((xnb, ynb, diag)):
        send(cown, call.at[i], tc.at[k], rc.at[i], (other, j))
    check = cown[...]
    for other in (xnb, ynb, diag):
        arrived(call.at[other], rc.at[other])
        check = check + call[other]
    chk_ref[...] = jnp.transpose(check / x_ref.shape[1])[0]

    for copy in sends:
        copy.wait_send()
    for copy in inner_sends:
        pl.when(inner)(copy.wait_send)
    for here, _, copy, _ in away_sends:
        pl.when(jnp.logical_not(here))(copy.wait_send)


def on_plane(saved_input, keep_bits, norm_gain, gate_weight, up_weight, down_weight):
    n, m = lax.axis_size("dp"), lax.axis_size("tensor")
    R, full = saved_input.shape
    width, U = gate_weight.shape
    TB = R * m
    out_rows = n * TB // m
    chips = m // 2
    lanes = -(-(keep_bits.shape[1] // m) // 128) * 128
    dma = pltpu.SemaphoreType.DMA
    vmem = pl.BlockSpec(memory_space=pltpu.VMEM)
    hbm = pl.BlockSpec(memory_space=pl.ANY)
    scratch = [
        pltpu.VMEM((width, U), BF16), pltpu.VMEM((width, U), BF16), pltpu.VMEM((U, width), BF16),
        pltpu.VMEM((n, m, R, width), BF16), pltpu.VMEM((n, TB, width), BF16),
        pltpu.VMEM((m, R, lanes), jnp.int32), pltpu.VMEM((m, R, lanes), jnp.int32),
        pltpu.VMEM((R, 128), F32), pltpu.VMEM((m, R, 128), F32), pltpu.VMEM((TB, U), F32),
        pltpu.VMEM((2, TB, U), BF16), pltpu.VMEM((2, TB, U), BF16), pltpu.VMEM((2, TB, U), BF16),
        pltpu.VMEM((2, TB, U), F32), pltpu.VMEM((2, TB, U), BF16),
        pltpu.VMEM((2, TB, U), BF16), pltpu.VMEM((2, TB, U), BF16),
        pltpu.VMEM((n, TB, U), BF16),
        pltpu.VMEM((n, 2, out_rows, width), F32), pltpu.VMEM((n, 2, out_rows, width), BF16),
        pltpu.VMEM((n, out_rows, width), BF16), pltpu.VMEM((n, out_rows, width), BF16),
        pltpu.VMEM((out_rows, width), F32), pltpu.VMEM((2, out_rows, width), BF16), pltpu.VMEM((n, out_rows, width), BF16),
        pltpu.VMEM((out_rows, 128), F32), pltpu.VMEM((n, out_rows, 128), F32),
        dma((3,)), dma((n, m)), dma((3,)), dma((n, 4)), dma((n, chips)),
        dma((m,)), dma((m - 1,)), dma((m,)), dma((m - 1,)),
        dma((COL_PARTS, 6)), dma((COL_PARTS, 6)), dma((n, COL_PARTS)), dma((COL_PARTS, 3)),
        dma((n, 2)), dma((n, 2)), dma((2, 2)), dma((n, 2)), dma((n, 2)), dma((n,)), dma((3,)),
    ]
    layer_out, check = pl.pallas_call(
        fused,
        out_shape=(
            jax.ShapeDtypeStruct((out_rows, width), BF16),
            jax.ShapeDtypeStruct((out_rows,), F32),
        ),
        in_specs=[vmem, vmem, vmem, hbm, hbm, hbm],
        out_specs=(vmem, vmem),
        scratch_shapes=scratch,
        compiler_params=pltpu.CompilerParams(
            collective_id=0, has_side_effects=True, vmem_limit_bytes=60 * 1024 * 1024
        ),
    )(saved_input, keep_bits, norm_gain, gate_weight, up_weight, down_weight)
    return layer_out, check


def solution(mesh):
    placed = (
        P(("dp", "tensor"), None),
        P(("dp", "tensor"), None),
        P("dp"),
        P("dp", "tensor"),
        P("dp", "tensor"),
        P("tensor", "dp"),
    )
    plane = mesh.shape["dp"] == 4 and mesh.shape["tensor"] == 2 * mesh.shape["dp"]
    return jax.shard_map(
        on_plane if plane else on_device,
        mesh=mesh,
        in_specs=placed,
        out_specs=(P("tensor", "dp"), P("tensor")),
        check_vma=False,
    )
```

profile of v0, /device:TPU:0, one launch (start us, length us, event | category | flops | bytes accessed | tf_op | source)
XLA Modules:
  0.0 100.8 jit_solution(4334184457626852068)
XLA Ops:
  0.6 97.3 %shard_map.77 = (bf16[64,2048]{1,0:T(8,128)(2,1)}, f32[64]{0:T(128)}) custom-call(bf16[16,8192]{1,0:T(8,128)(2,1)} %x_ref.1, s32[16,448]{1,0:T(8,128)} %kb_ref.1, bf16[2048]{0:T(1024)(128)(2,1)} %gain_ref.1, bf16[2048,1792]{1,0:T(8,128)(2,1)} %wg_hbm.1, bf16[2048,1792]{1,0:T(8,128)(2,1)} %wu_hbm.1, bf16[1792,2048]{1,0:T(8,128)(2,1)} %wd_hbm.1), custom_call_target="tpu_custom_call" | custom-call | tf_op jit(solution)/shard_map/pallas_call | solution.py:428
  98.0 1.7 %copy.10 = bf16[64,2048]{1,0:T(8,128)(2,1)} copy(bf16[64,2048]{1,0:T(8,128)(2,1)} %get-tuple-element.4) | data formatting | bytes 524288
  99.6 1.1 %copy.11 = f32[64]{0:T(128)} copy(f32[64]{0:T(128)} %get-tuple-element.5) | data formatting | bytes 512
where the time goes:
time: 101 us
  Pallas kernels  97.3 us (96%)
  local copies, waits for them, and re-layouts  2.8 us (3%)
    pallas_call x1, Pallas kernels, on_plane(): pl.pallas_call(fused, out_shape=(jax.ShapeDtypeStruct((out_rows, width),...  97.3 us
    unnamed x2, local copies, waits for them, and re-layouts  2.8 us

commit v1 on v0

v1 whole, which is shorter than its diff:
```python
import jax
import jax.numpy as jnp
from jax import lax
from jax.experimental import pallas as pl
from jax.experimental.pallas import tpu as pltpu
from jax.sharding import PartitionSpec as P

D = 8192


def on_device(saved_input, keep_bits, norm_gain, gate_weight, up_weight, down_weight):
    tensor_width = lax.axis_size("tensor")
    dp_width = lax.axis_size("dp")
    unit_words = lax.all_to_all(keep_bits, "tensor", split_axis=1, concat_axis=0, tiled=True)
    shifts = jnp.arange(32, dtype=jnp.int32)
    keep_mask = jnp.bitwise_and(jnp.right_shift(unit_words[:, :, None], shifts[None, None, :]), 1)
    keep_mask = keep_mask.reshape(unit_words.shape[0], -1)
    keep_scale = 2.0 * keep_mask.astype(jnp.float32)
    width_units = gate_weight.shape[1]
    columns = lax.all_to_all(saved_input, "dp", split_axis=1, concat_axis=0, tiled=True)
    collected = lax.all_gather(columns, "tensor", axis=0, tiled=True)
    per_device = saved_input.shape[0]
    collected = collected.reshape(tensor_width, dp_width, per_device, collected.shape[1])
    collected = collected.transpose(1, 0, 2, 3).reshape(-1, collected.shape[3])
    widened = collected.astype(jnp.float32)
    squares = lax.psum(jnp.sum(widened * widened, axis=1), "dp")
    inv_rms = lax.rsqrt(squares / D + 1e-05)
    normed = (widened * inv_rms[:, None] * norm_gain.astype(jnp.float32)[None, :]).astype(
        jnp.bfloat16
    )
    gate_part = jnp.dot(normed, gate_weight, preferred_element_type=jnp.float32)
    up_part = jnp.dot(normed, up_weight, preferred_element_type=jnp.float32)
    projected = lax.psum_scatter(
        jnp.concatenate((gate_part, up_part), axis=1).astype(jnp.bfloat16),
        "dp",
        scatter_dimension=0,
        tiled=True,
    ).astype(jnp.float32)
    gate_sum = projected[:, :width_units]
    up_sum = projected[:, width_units:]
    hidden = (jax.nn.silu(gate_sum) * up_sum * keep_scale).astype(jnp.bfloat16)
    partial_value = jnp.dot(
        lax.all_gather(hidden, "dp", axis=0, tiled=True),
        down_weight,
        preferred_element_type=jnp.float32,
    )
    mlp_sum = lax.psum_scatter(
        partial_value.astype(jnp.bfloat16), "tensor", scatter_dimension=0, tiled=True
    ).astype(jnp.float32)
    out_rows = mlp_sum.shape[0]
    first_row = lax.axis_index("tensor") * out_rows
    residual = lax.dynamic_slice_in_dim(collected, first_row, out_rows, 0)
    layer_out = (residual.astype(jnp.float32) + mlp_sum).astype(jnp.bfloat16)
    widened_out = layer_out.astype(jnp.float32)
    row_check = lax.psum(jnp.sum(widened_out * widened_out, axis=1), "dp") / D
    return (layer_out, row_check)


MESH = pl.DeviceIdType.MESH
F32 = jnp.float32
BF16 = jnp.bfloat16
WAVES = 4
COL_PARTS = 2


SCHEDULE = (
    ("own", 0), ("own", 1), ("ring", 0, 1), ("ring", 0, 2), ("ring", 0, 0), ("own", 2), ("gather", 0),
    ("project", 0, 0), ("ring", 1, 2), ("project", 0, 1), ("ring", 1, 1), ("ring", 1, 0), ("relay", 0, 0, 1),
    ("bits",), ("relay", 0, 0, 0), ("gather", 1), ("project", 1, 1), ("relay", 0, 1, 0), ("project", 1, 0),
    ("relay", 0, 1, 1), ("ring", 2, 1), ("ring", 2, 2), ("relay", 1, 1, 0), ("relay", 1, 1, 1), ("expand",),
    ("own", 3), ("relay", 1, 0, 0), ("activate", 0, 0), ("activate", 0, 1), ("ring", 2, 0), ("relay", 1, 0, 1),
    ("gather", 2), ("project", 2, 0), ("project", 2, 1), ("ring", 3, 2), ("relay", 2, 0, 1), ("ring", 3, 1),
    ("forward", 0, 1), ("forward", 0, 0), ("ring", 3, 0), ("activate", 1, 1), ("activate", 1, 0), ("gather", 3),
    ("project", 3, 0), ("relay", 2, 1, 0), ("down", 0, 0), ("forward", 1, 1), ("relay", 2, 0, 0), ("forward", 1, 0),
    ("relay", 2, 1, 1), ("relay", 3, 0, 0), ("pair", 0, 0), ("project", 3, 1), ("down", 0, 1), ("activate", 2, 1),
    ("relay", 3, 1, 0), ("pair", 0, 1), ("activate", 2, 0), ("down", 1, 0), ("relay", 3, 0, 1), ("relay", 3, 1, 1),
    ("forward", 2, 0), ("pair", 1, 0), ("down", 1, 1), ("forward", 2, 1), ("activate", 3, 0), ("activate", 3, 1),
    ("pair", 1, 1), ("down", 2, 0), ("forward", 3, 0), ("forward", 3, 1), ("join", 1, 0), ("join", 0, 1),
    ("down", 2, 1), ("pair", 2, 0), ("down", 3, 0), ("pair", 2, 1), ("down", 3, 1), ("join", 0, 0), ("pair", 3, 1),
    ("pair", 3, 0), ("join", 1, 1), ("join", 2, 1), ("join", 2, 0), ("finish", 0), ("join", 3, 1), ("join", 3, 0),
    ("finish", 1), ("finish", 2), ("finish", 3),
)


def fused(
    x_ref, kb_ref, gain_ref, wg_hbm, wu_hbm, wd_hbm, out_ref, chk_ref,
    wg, wu, wd, xs, xbuf, xn, kw, kall, iown, iall, word, rows_scale, keep,
    pb, hold, pown, relay, from_x, from_y, sums, hbuf, qf, qb, sib, ssend, jsend, zr, zpass, cown, csend, call,
    w_sem, rx, tx_dp, tx_z, tx_s, rk, tk, ri, ti, rp, tp, rh, th, rs, ts, rz, rpass, tz, tj, rc, tc,
):
    W, m, n, R, width = xbuf.shape
    U = wg.shape[1]
    TB = m * R
    half = TB // 2
    words = kb_ref.shape[1] // m
    tile = 256 if U % 256 == 0 and width % 256 == 0 else 128
    step_cols = -(-(U // tile) // COL_PARTS) * tile
    parts = tuple((lo, min(step_cols, U - lo)) for lo in range(0, U, step_cols))
    span = width // 2
    halves = [pl.ds(h * span, span) for h in range(2)]

    i, j = lax.axis_index("dp"), lax.axis_index("tensor")
    iy, ix = i // 2, i % 2
    z, c = j // 2, j % 2
    xnb = iy * 2 + (1 - ix)
    ynb = (1 - iy) * 2 + ix
    diag = (1 - iy) * 2 + (1 - ix)
    sibling = z * 2 + (1 - c)
    mate = z + 1 - 2 * (z % 2)
    far, far_end = 2 - z // 2, 3 * (1 - z // 2)
    away = 2 * (1 - z // 2)
    inner = (z + 1) // 2 == 1
    outer = (z + 1) // 2 != 1
    order = (diag, ynb, xnb, i)
    sends, inner_sends, outer_sends = [], [], []

    def remote(src, dst, ss, rsem, to):
        return pltpu.make_async_remote_copy(
            src_ref=src, dst_ref=dst, send_sem=ss, recv_sem=rsem, device_id=to, device_id_type=MESH
        )

    def send(src, dst, ss, rsem, to):
        copy = remote(src, dst, ss, rsem, to)
        copy.start()
        sends.append(copy)

    def arrived(dst, rsem):
        remote(dst, dst, tc.at[0], rsem, (i, sibling)).wait_recv()

    loads = [pltpu.make_async_copy(s, d, w_sem.at[k]) for k, (s, d) in enumerate(((wg_hbm, wg), (wu_hbm, wu), (wd_hbm, wd)))]
    for load in loads:
        load.start()

    barrier = pltpu.get_barrier_semaphore()
    for other in (xnb, ynb, diag):
        pl.semaphore_signal(barrier, inc=1, device_id=(other, j), device_id_type=MESH)
    for step in range(1, m):
        pl.semaphore_signal(barrier, inc=1, device_id=(i, (j + step) % m), device_id_type=MESH)
    for w in range(W):
        for b in range(n):
            xs[w, b] = x_ref[w * R : (w + 1) * R, b * width : (b + 1) * width]
        xbuf[w, j, i] = xs[w, i]
    pl.semaphore_wait(barrier, 3 + m - 1)

    for w in range(W):
        for k, other in enumerate((diag, ynb, xnb)):
            send(xs.at[w, other], xbuf.at[w, j, i], tx_dp.at[w, k], rx.at[w, j, k], (other, j))

    kw[...] = jnp.zeros_like(kw)
    for t in range(m):
        kw[t, :, 0:words] = kb_ref[:, t * words : (t + 1) * words]
    rows = x_ref[...].astype(F32)
    total = jnp.sum(rows * rows, axis=1, keepdims=True)
    iown[...] = jnp.broadcast_to(lax.rsqrt(total / (x_ref.shape[1]) + 1e-05), iown.shape)
    iall[j] = iown[...]
    kall[j] = kw[j]

    def own(w):
        for k, b in enumerate((diag, ynb, xnb)):
            arrived(xbuf.at[w, j, b], rx.at[w, j, k])
        for q, to in enumerate((far, mate)):
            send(xbuf.at[w, j], xbuf.at[w, j], tx_z.at[w, q], rx.at[w, j, 3], (i, to * 2 + c))
        send(xbuf.at[w, j], xbuf.at[w, j], tx_s.at[w, 0], rx.at[w, j, 3], (i, sibling))

    def ring(w, q):
        slot = (mate, far, far_end)[q] * 2 + c
        arrived(xbuf.at[w, slot], rx.at[w, slot, 3])
        if q > 0:
            copy = remote(xbuf.at[w, slot], xbuf.at[w, slot], tx_z.at[w, q + 1], rx.at[w, slot, 3], (i, mate * 2 + c))
            pl.when(inner)(copy.start)
            inner_sends.append(copy)
        send(xbuf.at[w, slot], xbuf.at[w, slot], tx_s.at[w, q + 1], rx.at[w, slot, 3], (i, sibling))

    gain = gain_ref[...].astype(F32).reshape(1, width)

    def gather(w):
        for chip in (z, mate, far, far_end):
            slot = chip * 2 + (1 - c)
            arrived(xbuf.at[w, slot], rx.at[w, slot, 3])
        for k, b in enumerate(order):
            for t in range(m):
                xn[w, k * TB + t * R : k * TB + (t + 1) * R, :] = (xbuf[w, t, b].astype(F32) * gain).astype(BF16)

    def bits():
        for step in range(1, m):
            to = (j + step) % m
            send(kw.at[to], kall.at[j], tk.at[step - 1], rk.at[j], (i, to))
            send(iown, iall.at[j], ti.at[step - 1], ri.at[j], (i, to))

    def expand():
        for step in range(1, m):
            slot = (j + step) % m
            arrived(kall.at[slot], rk.at[slot])
            arrived(iall.at[slot], ri.at[slot])
        lanes = kall.shape[2]
        for w in range(W):
            for t in range(m):
                at = (w * m + t) * R
                word[at : at + R, :] = kall[t, w * R : (w + 1) * R, :]
                rows_scale[at : at + R, :] = iall[t, w * R : (w + 1) * R, :]
        packed = word[...]
        byte = [jnp.bitwise_and(jnp.right_shift(packed, 8 * q), 255).astype(F32).astype(BF16) for q in range(4)]

        def body(t, carry):
            unit = t * tile + lax.broadcasted_iota(jnp.int32, (lanes, tile), 1)
            where = lax.broadcasted_iota(jnp.int32, (lanes, tile), 0)
            spread = jnp.zeros((W * TB, tile), F32)
            for q in range(4):
                hit = (jnp.right_shift(unit, 3) == where * 4 + q)
                spread += jnp.dot(byte[q], jnp.where(hit, 1.0, 0.0).astype(BF16), preferred_element_type=F32)
            shift = jnp.bitwise_and(lax.broadcasted_iota(jnp.int32, (W * TB, tile), 1), 7)
            bit = jnp.bitwise_and(jnp.right_shift(spread.astype(jnp.int32), shift), 1)
            keep[:, pl.ds(pl.multiple_of(t * tile, tile), tile)] = (2 * bit).astype(F32)
            return carry

        lax.fori_loop(0, U // tile, body, 0)

    def project(w, p):
        if w == 0 and p == 0:
            loads[0].wait()
            loads[1].wait()
        lo, size = parts[p]
        at = pl.ds(lo, size)
        for g, wt in enumerate((wg, wu)):

            def body(t, carry):
                cols = pl.ds(pl.multiple_of(t * tile, tile), tile)
                part = jnp.dot(xn[w], wt[:, cols], preferred_element_type=F32)
                direct, kept = (2, 1) if g == 0 else (1, 2)
                pb[w, g, 0, :, cols] = part[0:TB].astype(BF16)
                pb[w, g, 1, :, cols] = part[direct * TB : (direct + 1) * TB].astype(BF16)
                hold[w, g, :, cols] = part[kept * TB : (kept + 1) * TB]
                pown[w, g, :, cols] = part[3 * TB : 4 * TB]
                return carry

            lax.fori_loop(lo // tile, (lo + size) // tile, body, 0)
            to, land = ((xnb, from_x), (ynb, from_y))[g]
            send(pb.at[w, g, 0, :, at], relay.at[w, g, :, at], tp.at[w, p, 3 * g], rp.at[w, p, 3 * g], (to, j))
            send(pb.at[w, g, 1, :, at], land.at[w, g, :, at], tp.at[w, p, 3 * g + 1], rp.at[w, p, 3 * g + 1], (to, j))

    def pass_on(w, p, g):
        lo, size = parts[p]
        at = pl.ds(lo, size)
        arrived(relay.at[w, g, :, at], rp.at[w, p, 3 * g])
        sums[w, g, :, at] = (hold[w, g, :, at] + relay[w, g, :, at].astype(F32)).astype(BF16)
        to, land = ((ynb, from_y), (xnb, from_x))[g]
        send(sums.at[w, g, :, at], land.at[w, g, :, at], tp.at[w, p, 3 * g + 2], rp.at[w, p, 3 * g + 2], (to, j))

    def activate(w, p):
        lo, size = parts[p]
        at = pl.ds(lo, size)
        arrived(from_x.at[w, 0, :, at], rp.at[w, p, 1])
        arrived(from_y.at[w, 1, :, at], rp.at[w, p, 4])
        arrived(from_y.at[w, 0, :, at], rp.at[w, p, 2])
        arrived(from_x.at[w, 1, :, at], rp.at[w, p, 5])
        scale = rows_scale[w * TB : (w + 1) * TB, 0:1]
        gate = (pown[w, 0, :, at] + from_x[w, 0, :, at].astype(F32) + from_y[w, 0, :, at].astype(F32)) * scale
        up = (pown[w, 1, :, at] + from_x[w, 1, :, at].astype(F32) + from_y[w, 1, :, at].astype(F32)) * scale
        hbuf[w, i, :, at] = (gate / (1.0 + jnp.exp(-gate)) * up * keep[w * TB : (w + 1) * TB, lo : lo + size]).astype(BF16)
        send(hbuf.at[w, i, :, at], hbuf.at[w, i, :, at], th.at[w, p, 0], rh.at[w, i, p], (xnb, j))
        send(hbuf.at[w, i, :, at], hbuf.at[w, i, :, at], th.at[w, p, 1], rh.at[w, i, p], (ynb, j))

    def forward(w, p):
        lo, size = parts[p]
        at = pl.ds(lo, size)
        src, to = ((xnb, ynb), (ynb, xnb))[(p + w) % 2]
        arrived(hbuf.at[w, src, :, at], rh.at[w, src, p])
        send(hbuf.at[w, src, :, at], hbuf.at[w, src, :, at], th.at[w, p, 2], rh.at[w, src, p], (to, j))

    def down(w, h):
        if w == 0 and h == 0:
            loads[2].wait()
        if h == 0:
            for p, (lo, size) in enumerate(parts):
                at = pl.ds(lo, size)
                src = (ynb, xnb)[(p + w) % 2]
                arrived(hbuf.at[w, src, :, at], rh.at[w, src, p])
                arrived(hbuf.at[w, diag, :, at], rh.at[w, diag, p])

        def body(t, carry):
            cols = pl.ds(pl.multiple_of(t * tile, tile), tile)
            part = jnp.dot(hbuf[w].reshape(n * TB, U), wd[:, cols], preferred_element_type=F32)
            for b in range(n):
                for r in range(2):
                    piece = part[b * TB + r * half : b * TB + (r + 1) * half]
                    qf[w, r, b, :, cols] = piece
                    qb[w, r, b, :, cols] = piece.astype(BF16)
            return carry

        lax.fori_loop(h * span // tile, (h + 1) * span // tile, body, 0)
        at = halves[h]
        send(qb.at[w, 1 - c, :, :, at], sib.at[w, :, :, at], ts.at[w, h], rs.at[w, h], (i, sibling))

    def pair(w, h):
        at = halves[h]
        arrived(sib.at[w, :, :, at], rs.at[w, h])
        both = qf[w, c, :, :, at] + sib[w, :, :, at].astype(F32)
        qf[w, c, :, :, at] = both
        ssend[w, :, :, at] = both.astype(BF16)
        passed = remote(
            ssend.at[w, pl.ds(away, 2), :, at], zpass.at[w, :, :, at], tj.at[w, h, 0], rpass.at[w, h], (i, mate * 2 + c)
        )
        pl.when(outer)(passed.start)
        outer_sends.append(passed)
        send(ssend.at[w, mate, :, at], zr.at[w, 0, :, at], tz.at[w, h], rz.at[w, 0, h], (i, mate * 2 + c))

    def join(w, h):
        at = halves[h]
        copies = [
            remote(
                jsend.at[w, q, :, at], zr.at[w, 1, :, at], tj.at[w, h, q], rz.at[w, 1, h], (i, (away + q) * 2 + c)
            )
            for q in range(2)
        ]

        @pl.when(inner)
        def _():
            arrived(zpass.at[w, :, :, at], rpass.at[w, h])
            for q in range(2):
                jsend[w, q, :, at] = (qf[w, c, away + q, :, at] + zpass[w, q, :, at].astype(F32)).astype(BF16)
                copies[q].start()

        inner_sends.extend(copies)

    def finish(w):
        value = qf[w, c, z]
        for slot in range(2):
            for h in range(2):
                arrived(zr.at[w, slot, :, halves[h]], rz.at[w, slot, h])
            value = value + zr[w, slot].astype(F32)
        qf[w, c, z] = value
        for q in range(half // R):
            result = (xbuf[w, (half // R) * c + q, z].astype(F32) + qf[w, c, z, q * R : (q + 1) * R, :]).astype(BF16)
            at = (q * W + w) * R
            out_ref[at : at + R, :] = result
            wide = result.astype(F32)
            cown[at : at + R, :] = jnp.broadcast_to(jnp.sum(wide * wide, axis=1, keepdims=True), (R, cown.shape[1]))

    table = {
        "own": own, "ring": ring, "gather": gather, "bits": bits, "expand": expand, "project": project, "relay": pass_on,
        "activate": activate, "forward": forward, "down": down, "pair": pair, "join": join, "finish": finish,
    }
    for name, *step in SCHEDULE:
        table[name](*step)

    csend[...] = jnp.transpose(cown[...])[0:8, :]
    for k, other in enumerate((xnb, ynb, diag)):
        send(csend, call.at[i], tc.at[k], rc.at[i], (other, j))
    check = csend[...]
    for other in (xnb, ynb, diag):
        arrived(call.at[other], rc.at[other])
        check = check + call[other]
    chk_ref[...] = check[0] / x_ref.shape[1]

    for copy in sends:
        copy.wait_send()
    for copy in inner_sends:
        pl.when(inner)(copy.wait_send)
    for copy in outer_sends:
        pl.when(outer)(copy.wait_send)


def on_plane(saved_input, keep_bits, norm_gain, gate_weight, up_weight, down_weight):
    n, m = lax.axis_size("dp"), lax.axis_size("tensor")
    rows, full = saved_input.shape
    width, U = gate_weight.shape
    W = WAVES
    R = rows // W
    TB = R * m
    half = TB // 2
    out_rows = n * rows
    lanes = -(-(keep_bits.shape[1] // m) // 128) * 128
    P2 = COL_PARTS
    dma = pltpu.SemaphoreType.DMA
    vmem = pl.BlockSpec(memory_space=pltpu.VMEM)
    hbm = pl.BlockSpec(memory_space=pl.ANY)
    V = pltpu.VMEM
    scratch = [
        V((width, U), BF16), V((width, U), BF16), V((U, width), BF16),
        V((W, n, R, width), BF16), V((W, m, n, R, width), BF16), V((W, n * TB, width), BF16),
        V((m, rows, lanes), jnp.int32), V((m, rows, lanes), jnp.int32),
        V((rows, 128), F32), V((m, rows, 128), F32), V((W * TB, lanes), jnp.int32), V((W * TB, 128), F32), V((W * TB, U), F32),
        V((W, 2, 2, TB, U), BF16), V((W, 2, TB, U), F32), V((W, 2, TB, U), F32),
        V((W, 2, TB, U), BF16), V((W, 2, TB, U), BF16), V((W, 2, TB, U), BF16), V((W, 2, TB, U), BF16),
        V((W, n, TB, U), BF16),
        V((W, 2, n, half, width), F32), V((W, 2, n, half, width), BF16),
        V((W, n, half, width), BF16), V((W, n, half, width), BF16), V((W, 2, half, width), BF16),
        V((W, 2, half, width), BF16), V((W, 2, half, width), BF16),
        V((out_rows, 128), F32), V((8, out_rows), F32), V((n, 8, out_rows), F32),
        dma((3,)), dma((W, m, 4)), dma((W, 3)), dma((W, 4)), dma((W, 4)),
        dma((m,)), dma((m - 1,)), dma((m,)), dma((m - 1,)),
        dma((W, P2, 6)), dma((W, P2, 6)), dma((W, n, P2)), dma((W, P2, 3)),
        dma((W, 2)), dma((W, 2)), dma((W, 2, 2)), dma((W, 2)), dma((W, 2)), dma((W, 2, 2)), dma((n,)), dma((3,)),
    ]
    layer_out, check = pl.pallas_call(
        fused,
        out_shape=(
            jax.ShapeDtypeStruct((out_rows, width), BF16),
            jax.ShapeDtypeStruct((out_rows,), F32),
        ),
        in_specs=[vmem, vmem, vmem, hbm, hbm, hbm],
        out_specs=(vmem, vmem),
        scratch_shapes=scratch,
        compiler_params=pltpu.CompilerParams(
            collective_id=0, has_side_effects=True, vmem_limit_bytes=60 * 1024 * 1024
        ),
    )(saved_input, keep_bits, norm_gain, gate_weight, up_weight, down_weight)
    return layer_out, check


def solution(mesh):
    placed = (
        P(("dp", "tensor"), None),
        P(("dp", "tensor"), None),
        P("dp"),
        P("dp", "tensor"),
        P("dp", "tensor"),
        P("tensor", "dp"),
    )
    plane = mesh.shape["dp"] == 4 and mesh.shape["tensor"] == 2 * mesh.shape["dp"]
    return jax.shard_map(
        on_plane if plane else on_device,
        mesh=mesh,
        in_specs=placed,
        out_specs=(P("tensor", "dp"), P("tensor")),
        check_vma=False,
    )
```

time: 101 us -> 93.9 us (0.930)
  Pallas kernels: 97.3 us -> 90.3 us
    pallas_call x1, Pallas kernels: 97.3 us -> 90.3 us  [on_plane(): pl.pallas_call(fused, out_shape=(jax.ShapeDtypeStruct((out_rows, width),...]
where the time goes in v1:
time: 93.9 us; the launch traced here: 93.8 us
  Pallas kernels  90.3 us (96%)
  local copies, waits for them, and re-layouts  2.8 us (3%)
    pallas_call x1, Pallas kernels, on_plane(): pl.pallas_call(fused, out_shape=(jax.ShapeDtypeStruct((out_rows, width),...  90.3 us
    unnamed x2, local copies, waits for them, and re-layouts  2.8 us

profile of v1, /device:TPU:0, one launch (start us, length us, event | category | flops | bytes accessed | tf_op | source)
XLA Modules:
  0.0 93.8 jit_solution(7837859850973784574)
XLA Ops:
  0.6 90.3 %shard_map.77 = (bf16[64,2048]{1,0:T(8,128)(2,1)}, f32[64]{0:T(128)}) custom-call(bf16[16,8192]{1,0:T(8,128)(2,1)} %x_ref.1, s32[16,448]{1,0:T(8,128)} %kb_ref.1, bf16[2048]{0:T(1024)(128)(2,1)} %gain_ref.1, bf16[2048,1792]{1,0:T(8,128)(2,1)} %wg_hbm.1, bf16[2048,1792]{1,0:T(8,128)(2,1)} %wu_hbm.1, bf16[1792,2048]{1,0:T(8,128)(2,1)} %wd_hbm.1), custom_call_target="tpu_custom_call" | custom-call | tf_op jit(solution)/shard_map/pallas_call | solution.py:395
  91.0 1.7 %copy.10 = bf16[64,2048]{1,0:T(8,128)(2,1)} copy(bf16[64,2048]{1,0:T(8,128)(2,1)} %get-tuple-element.4) | data formatting | bytes 524288
  92.6 1.1 %copy.11 = f32[64]{0:T(128)} copy(f32[64]{0:T(128)} %get-tuple-element.5) | data formatting | bytes 512

commit v2 on v1

v2 whole, which is shorter than its diff:
```python
import jax
import jax.numpy as jnp
from jax import lax
from jax.experimental import pallas as pl
from jax.experimental.pallas import tpu as pltpu
from jax.sharding import PartitionSpec as P

D = 8192


def on_device(saved_input, keep_bits, norm_gain, gate_weight, up_weight, down_weight):
    tensor_width = lax.axis_size("tensor")
    dp_width = lax.axis_size("dp")
    unit_words = lax.all_to_all(keep_bits, "tensor", split_axis=1, concat_axis=0, tiled=True)
    shifts = jnp.arange(32, dtype=jnp.int32)
    keep_mask = jnp.bitwise_and(jnp.right_shift(unit_words[:, :, None], shifts[None, None, :]), 1)
    keep_mask = keep_mask.reshape(unit_words.shape[0], -1)
    keep_scale = 2.0 * keep_mask.astype(jnp.float32)
    width_units = gate_weight.shape[1]
    columns = lax.all_to_all(saved_input, "dp", split_axis=1, concat_axis=0, tiled=True)
    collected = lax.all_gather(columns, "tensor", axis=0, tiled=True)
    per_device = saved_input.shape[0]
    collected = collected.reshape(tensor_width, dp_width, per_device, collected.shape[1])
    collected = collected.transpose(1, 0, 2, 3).reshape(-1, collected.shape[3])
    widened = collected.astype(jnp.float32)
    squares = lax.psum(jnp.sum(widened * widened, axis=1), "dp")
    inv_rms = lax.rsqrt(squares / D + 1e-05)
    normed = (widened * inv_rms[:, None] * norm_gain.astype(jnp.float32)[None, :]).astype(
        jnp.bfloat16
    )
    gate_part = jnp.dot(normed, gate_weight, preferred_element_type=jnp.float32)
    up_part = jnp.dot(normed, up_weight, preferred_element_type=jnp.float32)
    projected = lax.psum_scatter(
        jnp.concatenate((gate_part, up_part), axis=1).astype(jnp.bfloat16),
        "dp",
        scatter_dimension=0,
        tiled=True,
    ).astype(jnp.float32)
    gate_sum = projected[:, :width_units]
    up_sum = projected[:, width_units:]
    hidden = (jax.nn.silu(gate_sum) * up_sum * keep_scale).astype(jnp.bfloat16)
    partial_value = jnp.dot(
        lax.all_gather(hidden, "dp", axis=0, tiled=True),
        down_weight,
        preferred_element_type=jnp.float32,
    )
    mlp_sum = lax.psum_scatter(
        partial_value.astype(jnp.bfloat16), "tensor", scatter_dimension=0, tiled=True
    ).astype(jnp.float32)
    out_rows = mlp_sum.shape[0]
    first_row = lax.axis_index("tensor") * out_rows
    residual = lax.dynamic_slice_in_dim(collected, first_row, out_rows, 0)
    layer_out = (residual.astype(jnp.float32) + mlp_sum).astype(jnp.bfloat16)
    widened_out = layer_out.astype(jnp.float32)
    row_check = lax.psum(jnp.sum(widened_out * widened_out, axis=1), "dp") / D
    return (layer_out, row_check)


MESH = pl.DeviceIdType.MESH
F32 = jnp.float32
BF16 = jnp.bfloat16
COL_PARTS = (4, 2, 2, 4)
SPLIT_LAST = (False, False, False, True)
SENDS = 48


SCHEDULE = (
    ("bits",), ("expand", 0), ("own", 0), ("own", 1), ("spread", 0), ("gather", 0), ("project", 0, 1),
    ("project", 0, 2), ("project", 0, 0), ("project", 0, 3), ("ring", 1, 0), ("ring", 1, 1), ("relay", 0, 1, 1),
    ("relay", 0, 1, 0), ("gather", 1), ("relay", 0, 2, 1), ("relay", 0, 0, 0), ("spread", 1), ("relay", 0, 0, 1),
    ("relay", 0, 2, 0), ("project", 1, 1), ("activate", 0, 1), ("expand", 1), ("relay", 0, 3, 1), ("relay", 0, 3, 0),
    ("activate", 0, 2), ("activate", 0, 0), ("project", 1, 0), ("forward", 0, 0), ("relay", 1, 1, 1),
    ("activate", 0, 3), ("relay", 1, 1, 0), ("ring", 3, 1), ("ring", 3, 0), ("forward", 0, 2), ("ring", 2, 0),
    ("gather", 3), ("forward", 0, 1), ("relay", 1, 0, 0), ("project", 3, 2), ("relay", 1, 0, 1), ("project", 3, 3),
    ("ring", 2, 1), ("forward", 0, 3), ("activate", 1, 1), ("project", 3, 0), ("relay", 3, 2, 0), ("gather", 2),
    ("activate", 1, 0), ("project", 2, 0), ("forward", 1, 1), ("down", 0, 0, 0), ("forward", 1, 0), ("project", 2, 1),
    ("relay", 2, 0, 0), ("down", 0, 0, 1), ("pair", 0, 0), ("relay", 2, 0, 1), ("relay", 2, 1, 0), ("relay", 2, 1, 1),
    ("project", 3, 1), ("down", 1, 0, 0), ("relay", 3, 0, 0), ("activate", 2, 0), ("pair", 1, 0), ("relay", 3, 3, 1),
    ("down", 1, 0, 1), ("activate", 2, 1), ("pair", 0, 1), ("relay", 3, 3, 0), ("relay", 3, 1, 0), ("relay", 3, 0, 1),
    ("join", 0, 0), ("relay", 3, 1, 1), ("relay", 3, 2, 1), ("forward", 2, 0), ("forward", 2, 1), ("activate", 3, 0),
    ("join", 1, 0), ("activate", 3, 1), ("pair", 1, 1), ("activate", 3, 2), ("activate", 3, 3), ("forward", 3, 0),
    ("join", 0, 1), ("down", 2, 0, 0), ("forward", 3, 2), ("join", 1, 1), ("forward", 3, 1), ("down", 2, 0, 1),
    ("forward", 3, 3), ("pair", 2, 0), ("down", 3, 0, 0), ("down", 3, 1, 0), ("pair", 2, 1), ("down", 3, 0, 1),
    ("join", 2, 0), ("down", 3, 1, 1), ("pair", 3, 1), ("pair", 3, 0), ("join", 2, 1), ("join", 3, 1), ("join", 3, 0),
    ("finish", 0), ("finish", 1), ("finish", 3), ("finish", 2),
)


def fused(
    x_hbm, kb_hbm, gain_hbm, wg_hbm, wu_hbm, wd_hbm, out_hbm, chk_hbm,
    x_ref, kb_ref, gain_ref, wg, wu, wd, xbuf, xn, kw, kall, iown, iall, word, rows_scale, keep,
    pb, hold, pown, relay, land, sums, hbuf, qf, qb, sib, ssend, jsend, zr, zpass,
    oown, osend, cown, csend, call, cout,
    w_sem, in_sem, out_sem, tx, rx, rs_x, rz_x, rk, rp, rf, rh, rs, rz, rpass, ro, rc,
):
    m, n, R, width = xbuf.shape
    W = m // 2
    U = wg.shape[1]
    TB = 2 * R
    out_rows = out_hbm.shape[0]
    words = kb_ref.shape[1] // m
    tile = 256 if U % 256 == 0 and width % 256 == 0 else 128
    span = width // 2
    halves = [pl.ds(h * span, span) for h in range(2)]

    def cut(pieces):
        step = -(-(U // tile) // pieces) * tile
        return tuple((lo, min(step, U - lo)) for lo in range(0, U, step))

    parts = [cut(pieces) for pieces in COL_PARTS]
    base = [sum(COL_PARTS[:w]) for w in range(W)]

    i, j = lax.axis_index("dp"), lax.axis_index("tensor")
    iy, ix = i // 2, i % 2
    z, c = j // 2, j % 2
    xnb = iy * 2 + (1 - ix)
    ynb = (1 - iy) * 2 + ix
    diag = (1 - iy) * 2 + (1 - ix)
    sibling = z * 2 + (1 - c)
    mate = z + 1 - 2 * (z % 2)
    far, far_end = 2 - z // 2, 3 * (1 - z // 2)
    within = (z + 1) // 2
    inner, outer = within == 1, within != 1
    within = within % 2
    planes = (z, mate, far, far_end)
    order = (diag, ynb, xnb, i)
    pending = [None] * SENDS
    count = [0]

    def settle(at):
        if pending[at] is not None:
            when, copy = pending[at]
            if when is None:
                copy.wait_send()
            else:
                pl.when(when)(copy.wait_send)
            pending[at] = None

    def send(src, dst, rsem, to, when=None):
        at = count[0] % SENDS
        count[0] += 1
        settle(at)
        copy = pltpu.make_async_remote_copy(
            src_ref=src, dst_ref=dst, send_sem=tx.at[at], recv_sem=rsem, device_id=to, device_id_type=MESH
        )
        pending[at] = (when, copy)
        if when is None:
            copy.start()
        else:
            pl.when(when)(copy.start)

    def arrived(dst, rsem):
        pltpu.make_async_remote_copy(
            src_ref=dst, dst_ref=dst, send_sem=tx.at[0], recv_sem=rsem, device_id=(i, sibling), device_id_type=MESH
        ).wait_recv()

    fetch = [pltpu.make_async_copy(s, d, in_sem.at[k]) for k, (s, d) in enumerate(((x_hbm, x_ref), (kb_hbm, kb_ref), (gain_hbm, gain_ref)))]
    for copy in fetch:
        copy.start()
    barrier = pltpu.get_barrier_semaphore()
    for other in (xnb, ynb, diag):
        pl.semaphore_signal(barrier, inc=1, device_id=(other, j), device_id_type=MESH)
    for step in range(1, m):
        pl.semaphore_signal(barrier, inc=1, device_id=(i, (j + step) % m), device_id_type=MESH)
    loads = [pltpu.make_async_copy(s, d, w_sem.at[k]) for k, (s, d) in enumerate(((wg_hbm, wg), (wu_hbm, wu), (wd_hbm, wd)))]
    for load in loads:
        load.start()
    for copy in fetch:
        copy.wait()
    xbuf[j, i] = x_ref[:, pl.ds(pl.multiple_of(i * width, width), width)]
    kw[...] = jnp.zeros_like(kw)
    for t in range(m):
        kw[t, :, 0:words] = kb_ref[:, t * words : (t + 1) * words]
    cown[...] = jnp.zeros_like(cown)
    pl.semaphore_wait(barrier, 3 + m - 1)

    for k, other in enumerate((xnb, diag, ynb)):
        send(x_ref.at[:, pl.ds(pl.multiple_of(other * width, width), width)], xbuf.at[j, i], rx.at[(k + 1) // 2], (other, j))

    rows = x_ref[...].astype(F32)
    total = jnp.sum(rows * rows, axis=1, keepdims=True)
    iown[...] = jnp.broadcast_to(lax.rsqrt(total / (x_ref.shape[1]) + 1e-05), iown.shape)
    iall[j] = iown[...]
    kall[j] = kw[j]

    pair_at = (2 * iy, 2 * (1 - iy))

    def own(h):
        arrived(xbuf.at[j, pl.ds(pair_at[h], 1 + h)], rx.at[h])
        block = xbuf.at[j, pl.ds(pair_at[h], 2)]
        send(block, block, rs_x.at[0], (i, sibling))
        send(block, block, rz_x.at[0, h], (i, mate * 2 + c))

    def spread(h):
        block = xbuf.at[j, pl.ds(pair_at[h], 2)]
        send(block, block, rz_x.at[2, h], (i, far_end * 2 + c), outer)
        send(block, block, rz_x.at[2 - within, h], (i, far * 2 + c))

    def ring(w, h):
        block = xbuf.at[planes[w] * 2 + c, pl.ds(pair_at[h], 2)]
        arrived(block, rz_x.at[w - 1, h])
        if w == 2:
            send(block, block, rz_x.at[1, h], (i, mate * 2 + c), inner)
        send(block, block, rs_x.at[w], (i, sibling))

    gain = gain_ref[...].astype(F32).reshape(1, width)

    def gather(w):
        other, mine = planes[w] * 2 + (1 - c), planes[w] * 2
        arrived(xbuf.at[other], rs_x.at[w])
        for k, b in enumerate(order):
            for t in range(2):
                at = k * TB + t * R
                xn[w, at : at + R, :] = (xbuf[mine + t, b].astype(F32) * gain).astype(BF16)

    def bits():
        for step in range(1, m):
            to = (j + step) % m
            kind = jnp.where(to == sibling, 0, 1)
            send(kw.at[to], kall.at[j], rk.at[0, kind], (i, to))
            send(iown, iall.at[j], rk.at[1, kind], (i, to))

    def expand(rest):
        first, waves = (1, W - 1) if rest else (0, 1)
        arrived(kall.at[0 : m - 2] if rest else kall.at[0], rk.at[0, rest])
        arrived(iall.at[0 : m - 2] if rest else iall.at[0], rk.at[1, rest])
        lanes = kall.shape[2]
        for w in range(first, first + waves):
            for t in range(2):
                at = w * TB + t * R
                word[at : at + R, :] = kall[planes[w] * 2 + t]
                rows_scale[at : at + R, :] = iall[planes[w] * 2 + t]
        lo, high = first * TB, (first + waves) * TB
        packed = word[lo:high, :]
        byte = [jnp.bitwise_and(jnp.right_shift(packed, 8 * q), 255).astype(F32).astype(BF16) for q in range(4)]

        def body(t, carry):
            unit = t * tile + lax.broadcasted_iota(jnp.int32, (lanes, tile), 1)
            where = lax.broadcasted_iota(jnp.int32, (lanes, tile), 0)
            spread_out = jnp.zeros((waves * TB, tile), F32)
            for q in range(4):
                hit = (jnp.right_shift(unit, 3) == where * 4 + q)
                spread_out += jnp.dot(byte[q], jnp.where(hit, 1.0, 0.0).astype(BF16), preferred_element_type=F32)
            shift = jnp.bitwise_and(lax.broadcasted_iota(jnp.int32, (waves * TB, tile), 1), 7)
            bit = jnp.bitwise_and(jnp.right_shift(spread_out.astype(jnp.int32), shift), 1)
            keep[lo:high, pl.ds(pl.multiple_of(t * tile, tile), tile)] = (2 * bit).astype(F32)
            return carry

        lax.fori_loop(0, U // tile, body, 0)

    loaded = [False] * 3

    def ready(k):
        if not loaded[k]:
            loads[k].wait()
        loaded[k] = True

    def project(w, p):
        ready(0)
        ready(1)
        lo, size = parts[w][p]
        at = pl.ds(lo, size)
        for g, wt in enumerate((wg, wu)):

            def body(t, carry):
                cols = pl.ds(pl.multiple_of(t * tile, tile), tile)
                part = jnp.dot(xn[w], wt[:, cols], preferred_element_type=F32)
                direct, kept = (2, 1) if g == 0 else (1, 2)
                pb[w, g, 0, :, cols] = part[0:TB].astype(BF16)
                pb[w, g, 1, :, cols] = part[direct * TB : (direct + 1) * TB].astype(BF16)
                hold[w, g, :, cols] = part[kept * TB : (kept + 1) * TB]
                pown[w, g, :, cols] = part[3 * TB : 4 * TB]
                return carry

            lax.fori_loop(lo // tile, (lo + size) // tile, body, 0)
            to = (xnb, ynb)[g]
            send(pb.at[w, g, 0, :, at], relay.at[w, g, :, at], rp.at[base[w] + p, g], (to, j))
            send(pb.at[w, g, 1, :, at], land.at[w, g, :, at], rp.at[base[w] + p, 2], (to, j))

    def pass_on(w, p, g):
        lo, size = parts[w][p]
        at = pl.ds(lo, size)
        arrived(relay.at[w, g, :, at], rp.at[base[w] + p, g])
        sums[w, g, :, at] = (hold[w, g, :, at] + relay[w, g, :, at].astype(F32)).astype(BF16)
        send(sums.at[w, g, :, at], land.at[w, 2 + g, :, at], rp.at[base[w] + p, 2], ((ynb, xnb)[g], j))

    def activate(w, p):
        lo, size = parts[w][p]
        at = pl.ds(lo, size)
        arrived(land.at[w, :, :, at], rp.at[base[w] + p, 2])
        scale = rows_scale[w * TB : (w + 1) * TB, 0:1]
        gate = (pown[w, 0, :, at] + land[w, 0, :, at].astype(F32) + land[w, 2, :, at].astype(F32)) * scale
        up = (pown[w, 1, :, at] + land[w, 1, :, at].astype(F32) + land[w, 3, :, at].astype(F32)) * scale
        hbuf[w, i, :, at] = (gate / (1.0 + jnp.exp(-gate)) * up * keep[w * TB : (w + 1) * TB, lo : lo + size]).astype(BF16)
        k = len(groups(w)) - 1 if p in groups(w)[-1] else 0
        rest = rh.at[w, k]
        for q, to in enumerate((xnb, ynb)):
            sem = rf.at[base[w] + p] if q == (p + w) % 2 else rest
            send(hbuf.at[w, i, :, at], hbuf.at[w, i, :, at], sem, (to, j))

    def forward(w, p):
        lo, size = parts[w][p]
        at = pl.ds(lo, size)
        src, to = ((xnb, ynb), (ynb, xnb))[(p + w) % 2]
        arrived(hbuf.at[w, src, :, at], rf.at[base[w] + p])
        k = len(groups(w)) - 1 if p in groups(w)[-1] else 0
        send(hbuf.at[w, src, :, at], hbuf.at[w, src, :, at], rh.at[w, k], (to, j))

    def groups(w):
        count = len(parts[w])
        return (range(count - 1), (count - 1,)) if SPLIT_LAST[w] else (range(count),)

    def down(w, k, h):
        ready(2)
        group = groups(w)[k]
        final = k == len(groups(w)) - 1
        low, top = parts[w][group[0]][0], sum(parts[w][group[-1]])
        if h == 0:
            arrived(hbuf.at[w, 0:2, :, pl.ds(low, top - low)], rh.at[w, k])

        def body(t, carry):
            cols = pl.ds(pl.multiple_of(t * tile, tile), tile)
            part = jnp.dot(
                hbuf[w, :, :, low:top].reshape(n * TB, top - low), wd[low:top, cols], preferred_element_type=F32
            )
            for b in range(n):
                for r in range(2):
                    piece = part[b * TB + r * R : b * TB + (r + 1) * R]
                    if k:
                        piece = piece + qf[w, r, b, :, cols]
                    qf[w, r, b, :, cols] = piece
                    if final:
                        qb[w, r, b, :, cols] = piece.astype(BF16)
            return carry

        lax.fori_loop(h * span // tile, (h + 1) * span // tile, body, 0)
        if final:
            at = halves[h]
            send(qb.at[w, 1 - c, :, :, at], sib.at[w, :, :, at], rs.at[w, h], (i, sibling))

    def pair(w, h):
        at, plane = halves[h], planes[w]
        arrived(sib.at[w, :, :, at], rs.at[w, h])
        both = qf[w, c, :, :, at] + sib[w, :, :, at].astype(F32)
        qf[w, c, :, :, at] = both
        ssend[w, :, :, at] = both.astype(BF16)
        send(ssend.at[w, far, :, at], zpass.at[plane, :, at], rpass.at[plane, h], (i, mate * 2 + c), outer)
        send(ssend.at[w, far_end, :, at], zr.at[plane, 1 + within, :, at], rz.at[plane], (i, far_end * 2 + c))
        send(ssend.at[w, mate, :, at], zr.at[plane, 0, :, at], rz.at[plane], (i, mate * 2 + c))

    def join(w, h):
        at = halves[h]
        mine = w if w > 1 else 1 - w
        plane = planes[mine]

        @pl.when(inner)
        def _():
            arrived(zpass.at[plane, :, at], rpass.at[plane, h])
            jsend[w, :, at] = (qf[mine, c, far, :, at] + zpass[plane, :, at].astype(F32)).astype(BF16)

        send(jsend.at[w, :, at], zr.at[plane, 1, :, at], rz.at[plane], (i, far * 2 + c), inner)

    def finish(k):
        w = (2, 1 - within, within, 3)[k]
        plane = (far, mate + within * (z - mate), z + within * (mate - z), far_end)[k]
        @pl.when(outer)
        def _():
            arrived(zr.at[plane], rz.at[plane])

        @pl.when(inner)
        def _():
            arrived(zr.at[plane, 0:2], rz.at[plane])

        value = qf[w, c, z] + zr[plane, 0].astype(F32) + zr[plane, 1].astype(F32)
        qf[w, c, z] = value

        @pl.when(outer)
        def _():
            qf[w, c, z] = qf[w, c, z] + zr[plane, 2].astype(F32)

        result = (xbuf[plane * 2 + c, z].astype(F32) + qf[w, c, z]).astype(BF16)
        wide = result.astype(F32)
        row = pl.multiple_of(plane * TB + c * R, R)
        cown[pl.ds(row, R), :] = jnp.broadcast_to(jnp.sum(wide * wide, axis=1, keepdims=True), (R, cown.shape[1]))
        osend[plane] = result
        here = plane // 2 == c
        slot = plane % 2

        @pl.when(here)
        def _():
            oown[2 * slot + c] = result

        send(osend.at[plane], oown.at[2 * slot + c], ro.at[0], (i, sibling), jnp.logical_not(here))

    table = {
        "own": own, "spread": spread, "ring": ring, "gather": gather, "bits": bits, "expand": expand, "project": project, "relay": pass_on,
        "activate": activate, "forward": forward, "down": down, "pair": pair, "join": join, "finish": finish,
    }
    for name, *step in SCHEDULE:
        table[name](*step)

    csend[...] = jnp.transpose(cown[...])[0:8, :]
    for k, other in enumerate((diag, xnb, ynb)):
        for t in range(2):
            send(csend, call.at[2 * k + c], rc.at[0], (other, z * 2 + t))
    send(csend, call.at[6], rc.at[0], (i, sibling))
    arrived(oown.at[0:2], ro.at[0])
    result_out = [pltpu.make_async_copy(oown.at[q], out_hbm.at[q * R : (q + 1) * R, :], out_sem.at[q]) for q in range(4)]
    for copy in result_out:
        copy.start()
    arrived(call, rc.at[0])
    check = csend[...]
    for k in range(7):
        check = check + call[k]
    check = check / x_ref.shape[1]
    cout[...] = jnp.where(c == 0, check[0, 0:out_rows], check[0, out_rows : 2 * out_rows])
    last_copy = pltpu.make_async_copy(cout, chk_hbm, out_sem.at[4])
    last_copy.start()

    for at in range(SENDS):
        settle(at)
    for copy in result_out:
        copy.wait()
    last_copy.wait()


def on_plane(saved_input, keep_bits, norm_gain, gate_weight, up_weight, down_weight):
    n, m = lax.axis_size("dp"), lax.axis_size("tensor")
    R, full = saved_input.shape
    width, U = gate_weight.shape
    W = m // 2
    TB = 2 * R
    out_rows = n * R
    lanes = -(-(keep_bits.shape[1] // m) // 128) * 128
    P2 = sum(COL_PARTS)
    dma = pltpu.SemaphoreType.DMA
    hbm = pl.BlockSpec(memory_space=pl.ANY)
    V = pltpu.VMEM
    scratch = [
        V((R, full), BF16), V(keep_bits.shape, jnp.int32), V((width,), BF16),
        V((width, U), BF16), V((width, U), BF16), V((U, width), BF16),
        V((m, n, R, width), BF16), V((W, n * TB, width), BF16),
        V((m, R, lanes), jnp.int32), V((m, R, lanes), jnp.int32),
        V((R, 128), F32), V((m, R, 128), F32), V((W * TB, lanes), jnp.int32), V((W * TB, 128), F32), V((W * TB, U), F32),
        V((W, 2, 2, TB, U), BF16), V((W, 2, TB, U), F32), V((W, 2, TB, U), F32),
        V((W, 2, TB, U), BF16), V((W, 4, TB, U), BF16), V((W, 2, TB, U), BF16),
        V((W, n, TB, U), BF16),
        V((W, 2, n, R, width), F32), V((W, 2, n, R, width), BF16),
        V((W, n, R, width), BF16), V((W, n, R, width), BF16), V((W, R, width), BF16),
        V((W, 3, R, width), BF16), V((W, R, width), BF16),
        V((n, R, width), BF16), V((W, R, width), BF16),
        V((W * TB, 128), F32), V((8, W * TB), F32), V((7, 8, W * TB), F32), V((out_rows,), F32),
        dma((3,)), dma((3,)), dma((5,)), dma((SENDS,)), dma((2,)), dma((W,)), dma((3, 2)), dma((2, 2)),
        dma((P2, 3)), dma((P2,)), dma((W, 2)), dma((W, 2)), dma((W,)), dma((W, 2)), dma((1,)), dma((1,)),
    ]
    layer_out, check = pl.pallas_call(
        fused,
        out_shape=(
            jax.ShapeDtypeStruct((out_rows, width), BF16),
            jax.ShapeDtypeStruct((out_rows,), F32),
        ),
        in_specs=[hbm] * 6,
        out_specs=(hbm, hbm),
        scratch_shapes=scratch,
        compiler_params=pltpu.CompilerParams(
            collective_id=0, has_side_effects=True, vmem_limit_bytes=60 * 1024 * 1024
        ),
    )(saved_input, keep_bits, norm_gain, gate_weight, up_weight, down_weight)
    return layer_out, check


def solution(mesh):
    placed = (
        P(("dp", "tensor"), None),
        P(("dp", "tensor"), None),
        P("dp"),
        P("dp", "tensor"),
        P("dp", "tensor"),
        P("tensor", "dp"),
    )
    plane = mesh.shape["dp"] == 4 and mesh.shape["tensor"] == 2 * mesh.shape["dp"]
    return jax.shard_map(
        on_plane if plane else on_device,
        mesh=mesh,
        in_specs=placed,
        out_specs=(P("tensor", "dp"), P("tensor")),
        check_vma=False,
    )
```

time: 93.9 us -> 84.8 us (0.903)
  Pallas kernels: 90.3 us -> 81.2 us
    pallas_call x1, Pallas kernels: 90.3 us -> 81.2 us  [on_plane(): pl.pallas_call(fused, out_shape=(jax.ShapeDtypeStruct((out_rows, width),...]
where the time goes in v2:
time: 84.8 us; the launch traced here: 84.6 us
  Pallas kernels  81.2 us (96%)
  local copies, waits for them, and re-layouts  2.8 us (3%)
    pallas_call x1, Pallas kernels, on_plane(): pl.pallas_call(fused, out_shape=(jax.ShapeDtypeStruct((out_rows, width),...  81.2 us
    unnamed x2, local copies, waits for them, and re-layouts  2.8 us

profile of v2, /device:TPU:0, one launch (start us, length us, event | category | flops | bytes accessed | tf_op | source)
XLA Modules:
  0.0 84.6 jit_solution(17957849447717160491)
XLA Ops:
  0.6 81.2 %shard_map.77 = (bf16[64,2048]{1,0:T(8,128)(2,1)}, f32[64]{0:T(128)}) custom-call(bf16[16,8192]{1,0:T(8,128)(2,1)} %x_hbm.1, s32[16,448]{1,0:T(8,128)} %kb_hbm.1, bf16[2048]{0:T(1024)(128)(2,1)} %gain_hbm.1, bf16[2048,1792]{1,0:T(8,128)(2,1)} %wg_hbm.1, bf16[2048,1792]{1,0:T(8,128)(2,1)} %wu_hbm.1, bf16[1792,2048]{1,0:T(8,128)(2,1)} %wd_hbm.1), custom_call_target="tpu_custom_call" | custom-call | tf_op jit(solution)/shard_map/pallas_call | solution.py:456
  81.8 1.7 %copy.10 = bf16[64,2048]{1,0:T(8,128)(2,1)} copy(bf16[64,2048]{1,0:T(8,128)(2,1)} %get-tuple-element.4) | data formatting | bytes 524288
  83.5 1.1 %copy.11 = f32[64]{0:T(128)} copy(f32[64]{0:T(128)} %get-tuple-element.5) | data formatting | bytes 512

commit v3 on v2

--- a/solution.py
+++ b/solution.py
@@ -87,17 +87,17 @@
 
 
 def fused(
-    x_hbm, kb_hbm, gain_hbm, wg_hbm, wu_hbm, wd_hbm, out_hbm, chk_hbm,
+    x_hbm, kb_hbm, gain_hbm, wg_hbm, wu_hbm, wd_hbm, out_ref, chk_ref,
     x_ref, kb_ref, gain_ref, wg, wu, wd, xbuf, xn, kw, kall, iown, iall, word, rows_scale, keep,
     pb, hold, pown, relay, land, sums, hbuf, qf, qb, sib, ssend, jsend, zr, zpass,
-    oown, osend, cown, csend, call, cout,
-    w_sem, in_sem, out_sem, tx, rx, rs_x, rz_x, rk, rp, rf, rh, rs, rz, rpass, ro, rc,
+    oown, osend, cown, csend, call,
+    w_sem, in_sem, tx, rx, rs_x, rz_x, rk, rp, rf, rh, rs, rz, rpass, ro, rc,
 ):
     m, n, R, width = xbuf.shape
     W = m // 2
     U = wg.shape[1]
     TB = 2 * R
-    out_rows = out_hbm.shape[0]
+    out_rows = out_ref.shape[0]
     words = kb_ref.shape[1] // m
     tile = 256 if U % 256 == 0 and width % 256 == 0 else 128
     span = width // 2
@@ -333,7 +333,7 @@
                         qb[w, r, b, :, cols] = piece.astype(BF16)
             return carry
 
-        lax.fori_loop(h * span // tile, (h + 1) * span // tile, body, 0)
+        lax.fori_loop(h * span // tile, (h + 1) * span // tile, body, 0, unroll=True)
         if final:
             at = halves[h]
             send(qb.at[w, 1 - c, :, :, at], sib.at[w, :, :, at], rs.at[w, h], (i, sibling))
@@ -405,23 +405,17 @@
             send(csend, call.at[2 * k + c], rc.at[0], (other, z * 2 + t))
     send(csend, call.at[6], rc.at[0], (i, sibling))
     arrived(oown.at[0:2], ro.at[0])
-    result_out = [pltpu.make_async_copy(oown.at[q], out_hbm.at[q * R : (q + 1) * R, :], out_sem.at[q]) for q in range(4)]
-    for copy in result_out:
-        copy.start()
+    for q in range(4):
+        out_ref[q * R : (q + 1) * R, :] = oown[q]
     arrived(call, rc.at[0])
     check = csend[...]
     for k in range(7):
         check = check + call[k]
     check = check / x_ref.shape[1]
-    cout[...] = jnp.where(c == 0, check[0, 0:out_rows], check[0, out_rows : 2 * out_rows])
-    last_copy = pltpu.make_async_copy(cout, chk_hbm, out_sem.at[4])
-    last_copy.start()
+    chk_ref[...] = jnp.where(c == 0, check[0, 0:out_rows], check[0, out_rows : 2 * out_rows])
 
     for at in range(SENDS):
         settle(at)
-    for copy in result_out:
-        copy.wait()
-    last_copy.wait()
 
 
 def on_plane(saved_input, keep_bits, norm_gain, gate_weight, up_weight, down_weight):
@@ -434,6 +428,7 @@
     lanes = -(-(keep_bits.shape[1] // m) // 128) * 128
     P2 = sum(COL_PARTS)
     dma = pltpu.SemaphoreType.DMA
+    vmem = pl.BlockSpec(memory_space=pltpu.VMEM)
     hbm = pl.BlockSpec(memory_space=pl.ANY)
     V = pltpu.VMEM
     scratch = [
@@ -449,18 +444,18 @@
         V((W, n, R, width), BF16), V((W, n, R, width), BF16), V((W, R, width), BF16),
         V((W, 3, R, width), BF16), V((W, R, width), BF16),
         V((n, R, width), BF16), V((W, R, width), BF16),
-        V((W * TB, 128), F32), V((8, W * TB), F32), V((7, 8, W * TB), F32), V((out_rows,), F32),
-        dma((3,)), dma((3,)), dma((5,)), dma((SENDS,)), dma((2,)), dma((W,)), dma((3, 2)), dma((2, 2)),
+        V((W * TB, 128), F32), V((8, W * TB), F32), V((7, 8, W * TB), F32),
+        dma((3,)), dma((3,)), dma((SENDS,)), dma((2,)), dma((W,)), dma((3, 2)), dma((2, 2)),
         dma((P2, 3)), dma((P2,)), dma((W, 2)), dma((W, 2)), dma((W,)), dma((W, 2)), dma((1,)), dma((1,)),
     ]
     layer_out, check = pl.pallas_call(
         fused,
         out_shape=(
-            jax.ShapeDtypeStruct((out_rows, width), BF16),
-            jax.ShapeDtypeStruct((out_rows,), F32),
+            pltpu.VMEM((out_rows, width), BF16),
+            pltpu.VMEM((out_rows,), F32),
         ),
         in_specs=[hbm] * 6,
-        out_specs=(hbm, hbm),
+        out_specs=(vmem, vmem),
         scratch_shapes=scratch,
         compiler_params=pltpu.CompilerParams(
             collective_id=0, has_side_effects=True, vmem_limit_bytes=60 * 1024 * 1024

time: 84.8 us -> 79.4 us (0.936)
  Pallas kernels: 81.2 us -> 77.4 us
  local copies, waits for them, and re-layouts: 2.8 us -> 1.22 us
    pallas_call x1, Pallas kernels: 81.2 us -> 77.4 us  [on_plane(): pl.pallas_call(fused, out_shape=(pltpu.VMEM((out_rows, width), BF16), plt...]
    unnamed x2, local copies, waits for them, and re-layouts: 2.8 us -> 1.22 us
where the time goes in v3:
time: 79.4 us; the launch traced here: 79.2 us
  Pallas kernels  77.4 us (97%)
  local copies, waits for them, and re-layouts  1.22 us (2%)
    pallas_call x1, Pallas kernels, on_plane(): pl.pallas_call(fused, out_shape=(pltpu.VMEM((out_rows, width), BF16), plt...  77.4 us

profile of v3, /device:TPU:0, one launch (start us, length us, event | category | flops | bytes accessed | tf_op | source)
XLA Modules:
  0.0 79.2 jit_solution(1322022529783777390)
XLA Ops:
  0.6 77.4 %shard_map.77 = (bf16[64,2048]{1,0:T(8,128)(2,1)S(1)}, f32[64]{0:T(128)S(1)}) custom-call(bf16[16,8192]{1,0:T(8,128)(2,1)} %x_hbm.1, s32[16,448]{1,0:T(8,128)} %kb_hbm.1, bf16[2048]{0:T(1024)(128)(2,1)} %gain_hbm.1, bf16[2048,1792]{1,0:T(8,128)(2,1)} %wg_hbm.1, bf16[2048,1792]{1,0:T(8,128)(2,1)} %wu_hbm.1, bf16[1792,2048]{1,0:T(8,128)(2,1)} %wd_hbm.1), custom_call_target="tpu_custom_call" | custom-call | tf_op jit(solution)/shard_map/pallas_call | solution.py:451
  78.0 0.7 copy.10
  78.7 0.5 copy.11

commit v4 on v3

--- a/solution.py
+++ b/solution.py
@@ -65,24 +65,25 @@
 
 
 SCHEDULE = (
-    ("bits",), ("expand", 0), ("own", 0), ("own", 1), ("spread", 0), ("gather", 0), ("project", 0, 1),
-    ("project", 0, 2), ("project", 0, 0), ("project", 0, 3), ("ring", 1, 0), ("ring", 1, 1), ("relay", 0, 1, 1),
-    ("relay", 0, 1, 0), ("gather", 1), ("relay", 0, 2, 1), ("relay", 0, 0, 0), ("spread", 1), ("relay", 0, 0, 1),
-    ("relay", 0, 2, 0), ("project", 1, 1), ("activate", 0, 1), ("expand", 1), ("relay", 0, 3, 1), ("relay", 0, 3, 0),
-    ("activate", 0, 2), ("activate", 0, 0), ("project", 1, 0), ("forward", 0, 0), ("relay", 1, 1, 1),
-    ("activate", 0, 3), ("relay", 1, 1, 0), ("ring", 3, 1), ("ring", 3, 0), ("forward", 0, 2), ("ring", 2, 0),
-    ("gather", 3), ("forward", 0, 1), ("relay", 1, 0, 0), ("project", 3, 2), ("relay", 1, 0, 1), ("project", 3, 3),
-    ("ring", 2, 1), ("forward", 0, 3), ("activate", 1, 1), ("project", 3, 0), ("relay", 3, 2, 0), ("gather", 2),
-    ("activate", 1, 0), ("project", 2, 0), ("forward", 1, 1), ("down", 0, 0, 0), ("forward", 1, 0), ("project", 2, 1),
-    ("relay", 2, 0, 0), ("down", 0, 0, 1), ("pair", 0, 0), ("relay", 2, 0, 1), ("relay", 2, 1, 0), ("relay", 2, 1, 1),
-    ("project", 3, 1), ("down", 1, 0, 0), ("relay", 3, 0, 0), ("activate", 2, 0), ("pair", 1, 0), ("relay", 3, 3, 1),
-    ("down", 1, 0, 1), ("activate", 2, 1), ("pair", 0, 1), ("relay", 3, 3, 0), ("relay", 3, 1, 0), ("relay", 3, 0, 1),
-    ("join", 0, 0), ("relay", 3, 1, 1), ("relay", 3, 2, 1), ("forward", 2, 0), ("forward", 2, 1), ("activate", 3, 0),
-    ("join", 1, 0), ("activate", 3, 1), ("pair", 1, 1), ("activate", 3, 2), ("activate", 3, 3), ("forward", 3, 0),
-    ("join", 0, 1), ("down", 2, 0, 0), ("forward", 3, 2), ("join", 1, 1), ("forward", 3, 1), ("down", 2, 0, 1),
-    ("forward", 3, 3), ("pair", 2, 0), ("down", 3, 0, 0), ("down", 3, 1, 0), ("pair", 2, 1), ("down", 3, 0, 1),
-    ("join", 2, 0), ("down", 3, 1, 1), ("pair", 3, 1), ("pair", 3, 0), ("join", 2, 1), ("join", 3, 1), ("join", 3, 0),
-    ("finish", 0), ("finish", 1), ("finish", 3), ("finish", 2),
+    ("bits",), ("own", 0), ("own", 1), ("spread", 0), ("gather", 0), ("spread", 1), ("project", 0, 0),
+    ("project", 0, 1), ("project", 0, 2), ("project", 0, 3), ("relay", 0, 0, 1), ("relay", 0, 1, 0), ("ring", 1, 0),
+    ("ring", 1, 1), ("expand", 0), ("relay", 0, 2, 0), ("gather", 1), ("relay", 0, 1, 1), ("relay", 0, 0, 0),
+    ("project", 1, 1), ("project", 1, 0), ("relay", 0, 2, 1), ("relay", 1, 1, 0), ("relay", 1, 1, 1), ("ring", 2, 0),
+    ("relay", 1, 0, 1), ("relay", 1, 0, 0), ("activate", 0, 1), ("ring", 3, 0), ("relay", 0, 3, 0),
+    ("relay", 0, 3, 1), ("expand", 1), ("activate", 0, 0), ("activate", 0, 2), ("ring", 3, 1), ("activate", 1, 1),
+    ("ring", 2, 1), ("gather", 3), ("activate", 1, 0), ("project", 3, 3), ("activate", 0, 3), ("forward", 1, 1),
+    ("forward", 0, 2), ("forward", 0, 1), ("project", 3, 2), ("gather", 2), ("project", 2, 1), ("forward", 1, 0),
+    ("project", 2, 0), ("relay", 2, 1, 0), ("relay", 2, 1, 1), ("project", 3, 1), ("relay", 2, 0, 0),
+    ("relay", 2, 0, 1), ("project", 3, 0), ("down", 1, 0, 0), ("down", 1, 0, 1), ("pair", 1, 1), ("forward", 0, 3),
+    ("relay", 3, 1, 0), ("relay", 3, 1, 1), ("forward", 0, 0), ("relay", 3, 3, 0), ("activate", 2, 1),
+    ("relay", 3, 2, 0), ("relay", 3, 2, 1), ("activate", 2, 0), ("relay", 3, 0, 1), ("down", 0, 0, 0),
+    ("relay", 3, 0, 0), ("pair", 1, 0), ("forward", 2, 1), ("activate", 3, 2), ("forward", 2, 0), ("pair", 0, 0),
+    ("relay", 3, 3, 1), ("down", 0, 0, 1), ("activate", 3, 0), ("activate", 3, 1), ("pair", 0, 1), ("activate", 3, 3),
+    ("join", 1, 0), ("forward", 3, 2), ("down", 2, 0, 0), ("forward", 3, 1), ("forward", 3, 0), ("join", 0, 0),
+    ("down", 2, 0, 1), ("join", 0, 1), ("pair", 2, 0), ("join", 1, 1), ("forward", 3, 3), ("down", 3, 0, 0),
+    ("pair", 2, 1), ("down", 3, 0, 1), ("join", 2, 0), ("down", 3, 1, 0), ("down", 3, 1, 1), ("pair", 3, 1),
+    ("pair", 3, 0), ("join", 2, 1), ("finish", 0), ("join", 3, 1), ("join", 3, 0), ("finish", 1), ("finish", 3),
+    ("finish", 2),
 )
 
 

time: 79.4 us -> 79.3 us (level)
  no operation moved by 1% of the time
where the time goes in v4:
time: 79.3 us; the launch traced here: 79.1 us
  Pallas kernels  77.3 us (97%)
  local copies, waits for them, and re-layouts  1.22 us (2%)
    pallas_call x1, Pallas kernels, on_plane(): pl.pallas_call(fused, out_shape=(pltpu.VMEM((out_rows, width), BF16), plt...  77.3 us

profile of v4, /device:TPU:0, one launch (start us, length us, event | category | flops | bytes accessed | tf_op | source)
XLA Modules:
  0.0 79.1 jit_solution(1252682664666578216)
XLA Ops:
  0.6 77.3 %shard_map.77 = (bf16[64,2048]{1,0:T(8,128)(2,1)S(1)}, f32[64]{0:T(128)S(1)}) custom-call(bf16[16,8192]{1,0:T(8,128)(2,1)} %x_hbm.1, s32[16,448]{1,0:T(8,128)} %kb_hbm.1, bf16[2048]{0:T(1024)(128)(2,1)} %gain_hbm.1, bf16[2048,1792]{1,0:T(8,128)(2,1)} %wg_hbm.1, bf16[2048,1792]{1,0:T(8,128)(2,1)} %wu_hbm.1, bf16[1792,2048]{1,0:T(8,128)(2,1)} %wd_hbm.1), custom_call_target="tpu_custom_call" | custom-call | tf_op jit(solution)/shard_map/pallas_call | solution.py:452
  77.9 0.7 copy.10
  78.6 0.5 copy.11
